TPU v7x, 32 devices: a whole 2x2x4 slice. The times are simulated.
32 devices in a mesh: section: 4 (over z), rep: 8 (over y, x, core).
Axes of the slice: x: 2, y: 2, z: 4, core: 2. Of those that a mesh axis runs over, the one named last changes fastest.
Arguments:
- cache: bfloat16 [4, 4096, 3584], P('section', 'rep'), may hold values from -6 to 6
- payload: bfloat16 [4, 4096, 3584], P('section', 'rep'), may hold values from -6 to 6
- block_ids: int32 [4, 8, 2], P('section', 'rep'), may hold values from 0 to 3, as said below
- block_counts: int32 [4, 8], P('section', 'rep'), may hold values from 1 to 2, as said below
- block_scales: int32 [4, 8, 2], P('section', 'rep'), may hold values from 1024 to 8192
- refresh_ids: int32 [4, 8, 128], P('section', 'rep'), may hold values from 0 to 511, as said below
- refresh_counts: int32 [4, 8], P('section', 'rep'), may hold values from 1 to 128, as said below
- norm_gain: float32 [4, 3584], P('section'), may hold values from 0.5 to 1.5
- query_weight: bfloat16 [4, 3584, 3584], P('section', 'rep'), may hold values from -0.09375 to 0.09375
- query_bias: float32 [4, 3584], P('section'), may hold values from -3 to 3
- kv_weight: bfloat16 [4, 3584, 1024], P('section', 'rep'), may hold values from -0.09375 to 0.09375
- kv_bias: float32 [4, 1024], P('section'), may hold values from -3 to 3
Outputs:
- rebuilt: bfloat16 [4, 4096, 3584], P('section', 'rep')
- queries: bfloat16 [4, 4096, 3584], P('section', 'rep')
- keys_values: bfloat16 [4, 4096, 1024], P('section', 'rep')
Inputs may be any that keep to these rules, and one draw needn't show every extreme that they name: `block_ids`: for each section and relay the 2 entries are different block numbers; only the first block_counts entries are used. `block_counts`: in every section some relay lists exactly 2 blocks. `refresh_ids`: for each section and relay the entries are different local row numbers; only the first refresh_counts entries are used. `refresh_counts`: in every section some relay lists exactly 128 rows.
All inputs are finite; a program needn't handle non-finite values.
Results may differ from a plain program's by a relative error of at most 0.0052.
Values may be sent and summed in bfloat16 or wider, within the bound.
A program may use at most 256 MiB of HBM per device.

v0:
```python
import functools

import jax
import jax.numpy as jnp
from jax import lax
from jax.experimental import pallas as pl
from jax.experimental.pallas import tpu as pltpu
from jax.sharding import PartitionSpec as P

BLK = 128
CW = 256
SLOT = 2
GW = SLOT * CW
TILE = 16
EPSILON = 1e-06
KERNEL_VMEM = 100 * 512 * 1024
OUT_VMEM = 3 * 1024 * 1024
MESH = pl.DeviceIdType.MESH


def chip_at(pos, chips):
    half = chips // 2
    back = pos // half
    return pos + back * (half + chips - 1 - 2 * pos)


def kernel(
    sections,
    reps,
    most_blk,
    lists_ref,
    payload_ref,
    cache_ref,
    gain_ref,
    qw_ref,
    qb_ref,
    kvw_ref,
    kvb_ref,
    rebuilt_ref,
    q_ref,
    kv_ref,
    last_w,
    last_normed,
    last_sums,
    w,
    normed,
    early,
    sums,
    values,
    bias,
    lists,
    local_sem,
    keep_sem,
    row_send,
    row_recv,
    own_send,
    pair_own_recv,
    ring_send,
    ring_recv,
    pair_send,
    pair_recv,
    far_send,
    far_recv,
    far_pair_send,
    far_pair_recv,
):
    chips = reps // 2
    hops = chips // 2
    depth = qw_ref.shape[1]
    rows = payload_ref.shape[1]
    feature = payload_ref.shape[2]
    ngq = qw_ref.shape[2] // GW
    ng = ngq + kvw_ref.shape[2] // GW
    nq = ngq * SLOT
    nc = ng * SLOT
    nh = nc // 2
    row_chunks = rows // BLK

    section = lax.axis_index("section")
    me = lax.axis_index("rep")
    core = me % 2
    chip = me // 2
    pos = chip + (chip // hops) * (hops + chips - 1 - 2 * chip)
    partner = 2 * chip + (1 - core)

    def rep_at(place, which):
        return 2 * chip_at((place + chips) % chips, chips) + which

    towards = (rep_at(pos + 1, core), rep_at(pos - 1, core))

    barrier = pltpu.get_barrier_semaphore()
    for other in towards + (partner,):
        pl.semaphore_signal(barrier, 1, device_id={"rep": other}, device_id_type=MESH)

    @pl.when(section > 0)
    def _():
        pl.semaphore_signal(
            barrier, 1, device_id={"section": section - 1}, device_id_type=MESH
        )

    @pl.when(section < sections - 1)
    def _():
        pl.semaphore_signal(
            barrier, 1, device_id={"section": section + 1}, device_id_type=MESH
        )

    def own(g):
        if g < ngq:
            return qw_ref.at[0, :, pl.ds(g * GW, GW)]
        return kvw_ref.at[0, :, pl.ds((g - ngq) * GW, GW)]

    def depth_of(block):
        return pl.ds(pl.multiple_of(block * depth, depth), depth)

    def columns_of(c):
        return pl.ds(pl.multiple_of((c % SLOT) * CW, CW), CW)

    def slot(g, block):
        return w.at[g, depth_of(block), :]

    def piece(c, block):
        return w.at[c // SLOT, depth_of(block), columns_of(c)]

    keep = pltpu.make_async_copy(cache_ref, rebuilt_ref, keep_sem)
    own_locals = [
        pltpu.make_async_copy(own(g), slot(g, me), local_sem.at[g]) for g in range(ng)
    ]

    sides = (section + sections - 1) // sections + (2 * sections - 2 - section) // sections
    pl.semaphore_wait(barrier, 3 + sides)

    def list_copy(i):
        return pltpu.make_async_remote_copy(
            src_ref=lists_ref[i],
            dst_ref=lists[i],
            send_sem=row_send.at[row_chunks + i],
            recv_sem=row_recv.at[row_chunks + i],
            device_id={"section": section + 1},
            device_id_type=MESH,
        )

    def row_copy(j):
        return pltpu.make_async_remote_copy(
            src_ref=payload_ref.at[0, pl.ds(j * BLK, BLK), :],
            dst_ref=values.at[pl.ds(j * BLK, BLK), :],
            send_sem=row_send.at[j],
            recv_sem=row_recv.at[j],
            device_id={"section": section + 1},
            device_id_type=MESH,
        )

    for g in range(ng):
        for d in range(2):
            pltpu.make_async_remote_copy(
                src_ref=own(g),
                dst_ref=slot(g, me),
                send_sem=own_send.at[d],
                recv_sem=ring_recv.at[d, 0, g],
                device_id={"rep": towards[d]},
                device_id_type=MESH,
            ).start()
        if g == 0:

            @pl.when(section < sections - 1)
            def _():
                for j in range(row_chunks):
                    row_copy(j).start()
                    if j == 0:
                        for i in range(len(lists)):
                            list_copy(i).start()

            keep.start()

        pltpu.make_async_remote_copy(
            src_ref=own(g),
            dst_ref=slot(g, me),
            send_sem=own_send.at[2],
            recv_sem=pair_own_recv.at[g],
            device_id={"rep": partner},
            device_id_type=MESH,
        ).start()
        own_locals[g].start()

    @pl.when(section == 0)
    def _():
        for ref in lists:
            ref[...] = jnp.zeros_like(ref)

        @pl.loop(0, rows // TILE)
        def _(i):
            values[pl.ds(i * TILE, TILE), :] = jnp.zeros((TILE, feature), values.dtype)

    for g in range(ngq):
        bias[g] = qb_ref[:, g * GW : (g + 1) * GW]
    for g in range(ngq, ng):
        bias[g] = kvb_ref[:, (g - ngq) * GW : (g - ngq + 1) * GW]
    keep.wait()
    for g in range(ng):
        own_locals[g].wait()

    def block_of(d, t, which):
        return rep_at(pos - t if d == 0 else pos + t, which)

    def landed(here, sem):
        pltpu.make_async_copy(here, here, sem).wait()

    def pass_on(here, send_sem, recv_sem, target):
        pltpu.make_async_remote_copy(
            src_ref=here,
            dst_ref=here,
            send_sem=send_sem,
            recv_sem=recv_sem,
            device_id={"rep": target},
            device_id_type=MESH,
        ).start()

    def rebuild(j):
        @pl.when(section > 0)
        def _():
            if j == 0:
                for i in range(len(lists)):
                    list_copy(i).wait_recv()
            row_copy(j).wait_recv()

        got_rows, got_ids, got_scales, got_counts, got_rcounts = lists
        count = got_counts[...]
        factor = jnp.zeros((1, 1), jnp.float32)
        for i in range(most_blk):
            live = jnp.logical_and(got_ids[:, i : i + 1] == j, count > i)
            scale = got_scales[:, i : i + 1].astype(jnp.float32) / 4096.0
            factor = factor + jnp.where(live, scale, 0.0)

        @pl.loop(0, BLK // TILE)
        def _(i):
            first = j * BLK + i * TILE
            here = pl.ds(pl.multiple_of(first, TILE), TILE)
            ids = got_rows[...]
            lanes = lax.broadcasted_iota(jnp.int32, ids.shape, 1)
            ids = jnp.where(lanes < got_rcounts[...], ids, -1)
            number = first + lax.broadcasted_iota(jnp.int32, (TILE, ids.shape[1]), 0)
            match = jnp.where(ids == number, 1.0, 0.0)
            hit = jnp.max(match, axis=1, keepdims=True) > 0.0
            got = values[here, :].astype(jnp.float32)
            delta = (got * factor).astype(jnp.bfloat16).astype(jnp.float32)
            mixed = jnp.where(hit, got, rebuilt_ref[0, here, :].astype(jnp.float32) + delta)
            rebuilt = mixed.astype(jnp.bfloat16)
            rebuilt_ref[0, here, :] = rebuilt
            wide = rebuilt.astype(jnp.float32)
            mean = jnp.sum(wide * wide, axis=1, keepdims=True) / feature
            scale_rows = lax.rsqrt(mean + EPSILON)
            result = (wide * scale_rows * gain_ref[...]).astype(jnp.bfloat16)
            for k in range(chips):
                normed[k, here, :] = result[:, 2 * depth * k : 2 * depth * (k + 1)]

    far = chip_at((pos + hops) % chips, chips)
    wide_depth = 2 * depth
    half = rows // 2

    def term(which, g, columns, first):
        rows_here = pl.ds(pl.multiple_of(which * wide_depth, wide_depth), wide_depth)
        return jnp.dot(
            normed[which, first : first + half, :],
            w[g, rows_here, columns],
            preferred_element_type=jnp.float32,
        )

    def near(g, columns, first):
        total = bias[g, :, columns]
        for step in range(1, chips):
            total = total + term((far + step) % chips, g, columns, first)
        return total

    def start(g):
        landed(slot(g, partner), pair_own_recv.at[g])
        for t in range(1, hops):
            for e in range(2):
                landed(slot(g, block_of(e, t, 1 - core)), pair_recv.at[e, t - 1, g])
        early[g] = near(g, slice(None), 0)

    marks = [(j + 1) * ng // row_chunks for j in range(row_chunks)]
    marks[-1] = ng
    ready = marks[row_chunks // 2 - 1]
    per_step = -(-ng // (ng - ready))
    for t in range(1, hops):
        done = 0
        for j, mark in enumerate(marks):

            @pl.loop(done, mark)
            def _(g):
                for d in range(2):
                    here = slot(g, block_of(d, t, core))
                    landed(here, ring_recv.at[d, t - 1, g])
                    if t + 1 < hops:
                        pass_on(here, ring_send.at[d, t - 1], ring_recv.at[d, t, g], towards[d])
                    else:
                        for k in range(SLOT):
                            c = g * SLOT + k
                            last = nh - 1 + d * nh

                            @pl.when((c < last) if d == 0 else ((c >= nh) & (c < last)))
                            def _():
                                pass_on(
                                    piece(c, block_of(d, t, core)),
                                    far_send.at[d],
                                    far_recv.at[d, c - d * nh],
                                    towards[d],
                                )

                            if k == last % SLOT:

                                @pl.when(c == last)
                                def _():
                                    pltpu.make_async_remote_copy(
                                        src_ref=w.at[
                                            last // SLOT,
                                            depth_of(block_of(d, t, core)),
                                            pl.ds(k * CW, CW),
                                        ],
                                        dst_ref=last_w.at[d, depth_of(core), :],
                                        send_sem=far_send.at[d],
                                        recv_sem=far_recv.at[d, nh - 1],
                                        device_id={"rep": towards[d]},
                                        device_id_type=MESH,
                                    ).start()

                    pass_on(here, pair_send.at[d, t - 1], pair_recv.at[d, t - 1, g], partner)
                if t + 1 == hops and (t > 1 or done >= ready):
                    for k in range(per_step):
                        other = (g - ready) * per_step + k

                        @pl.when(jnp.logical_and(other >= 0, other < ng))
                        def _():
                            start(other)

            done = mark
            if t == 1:
                rebuild(j)

    def partial(i):
        for d in range(2):
            c = i + d * nh
            sums[i % 2, d] = near(c // SLOT, columns_of(c), half)

    def paired(i):
        for d in range(2):
            c = i + d * nh
            landed(piece(c, block_of(d, hops, 1 - core)), far_pair_recv.at[d, i])

    def finish(i):
        for d in range(2):
            c = i + d * nh
            for first in (0, half):
                if first == 0:
                    total = early[c // SLOT, :, columns_of(c)]
                else:
                    total = sums[i % 2, d]
                total = total + term(far, c // SLOT, columns_of(c), first)
                result = total.astype(jnp.bfloat16)
                here = slice(first, first + half)

                @pl.when(c < nq)
                def _():
                    q_ref[0, here, pl.ds(pl.multiple_of(c * CW, CW), CW)] = result

                @pl.when(c >= nq)
                def _():
                    kv_ref[0, here, pl.ds(pl.multiple_of((c - nq) * CW, CW), CW)] = result

    def arrived(i):
        for d in range(2):
            c = i + d * nh
            here = piece(c, block_of(d, hops, core))
            landed(here, far_recv.at[d, i])
            pass_on(here, far_pair_send.at[d], far_pair_recv.at[d, i], partner)

    partial(0)
    last_normed[...] = normed[far]
    for d in range(2):
        c = nh - 1 + d * nh
        columns = slice((c % SLOT) * CW, (c % SLOT + 1) * CW)
        last_sums[d, :half, :] = early[c // SLOT, :, columns]
        last_sums[d, half:, :] = near(c // SLOT, columns, half)

    @pl.loop(0, nh - 1)
    def _(i):
        arrived(i)

        @pl.when(i + 1 < nh - 1)
        def _():
            partial(i + 1)

        paired(i)
        finish(i)

    for d in range(2):
        here = last_w.at[d, depth_of(core), :]
        landed(here, far_recv.at[d, nh - 1])
        pass_on(here, far_pair_send.at[d], far_pair_recv.at[d, nh - 1], partner)

    def sent(sem, count, width):
        part = w.at[pl.ds(0, count), pl.ds(0, depth), pl.ds(0, width)]
        pltpu.make_async_copy(part, part, sem).wait()

    for k in range(3):
        sent(own_send.at[k], ng, GW)
    for d in range(2):
        for t in range(1, hops):
            if t + 1 < hops:
                sent(ring_send.at[d, t - 1], ng, GW)
            sent(pair_send.at[d, t - 1], ng, GW)
        sent(far_send.at[d], ng, CW)

    @pl.when(section < sections - 1)
    def _():
        for i in range(len(lists)):
            list_copy(i).wait_send()
        for j in range(row_chunks):
            row_copy(j).wait_send()

    for d in range(2):
        sent(far_pair_send.at[d], ng, CW)
        landed(last_w.at[d, depth_of(1 - core), :], far_pair_recv.at[d, nh - 1])


def put_out(
    parts,
    rebuilt_ref,
    q_ref,
    kv_ref,
    last_w,
    last_normed,
    last_sums,
    rebuilt_out,
    q_out,
    kv_out,
    last,
    sem,
    last_sem,
):
    rows = q_ref.shape[1]
    nq = q_ref.shape[2] // CW
    nc = nq + kv_ref.shape[2] // CW
    last_pieces = (nc // 2 - 1, nc - 1)

    copies = []

    def out(source, target, first, stop):
        step = rows // parts
        for j in range(parts):
            here = pl.ds(j * step, step)
            columns = pl.ds(first, stop - first)
            copy = pltpu.make_async_copy(
                source.at[:, here, columns], target.at[:, here, columns], sem.at[len(copies)]
            )
            copy.start()
            copies.append(copy)

    out(rebuilt_ref, rebuilt_out, 0, rebuilt_ref.shape[2])
    for source, target, base in ((q_ref, q_out, 0), (kv_ref, kv_out, nq)):
        first = 0
        count = source.shape[2] // CW
        for c in last_pieces:
            if base <= c < base + count:
                if c - base > first:
                    out(source, target, first * CW, (c - base) * CW)
                first = c - base + 1
        if first < count:
            out(source, target, first * CW, count * CW)

    for d, c in enumerate(last_pieces):
        total = last_sums[d] + jnp.dot(
            last_normed[...], last_w[d], preferred_element_type=jnp.float32
        )
        last[d] = total.astype(jnp.bfloat16)
        target, base = (q_out, 0) if c < nq else (kv_out, nq)
        copy = pltpu.make_async_copy(
            last.at[d], target.at[0, :, pl.ds((c - base) * CW, CW)], last_sem.at[d]
        )
        copy.start()
        copies.append(copy)
    for copy in copies:
        copy.wait()


def body(
    cache,
    payload,
    block_ids,
    block_counts,
    block_scales,
    refresh_ids,
    refresh_counts,
    norm_gain,
    query_weight,
    query_bias,
    kv_weight,
    kv_bias,
):
    sections = lax.axis_size("section")
    reps = lax.axis_size("rep")
    rows, feature = cache.shape[1:]
    depth = query_weight.shape[1]
    queries = query_weight.shape[2]
    keys = kv_weight.shape[2]
    most_blk = block_ids.shape[2]
    ng = (queries + keys) // GW
    nh = ng * SLOT // 2
    hops = reps // 4
    row_chunks = rows // BLK

    lists = (refresh_ids[0], block_ids[0], block_scales[0], block_counts, refresh_counts)
    vmem = pl.BlockSpec(memory_space=pltpu.VMEM)
    anywhere = pl.BlockSpec(memory_space=pltpu.HBM)
    dma = pltpu.SemaphoreType.DMA
    results = pl.pallas_call(
        functools.partial(kernel, sections, reps, most_blk),
        out_shape=(
            pltpu.VMEM(cache.shape, cache.dtype),
            pltpu.VMEM((1, rows, queries), cache.dtype),
            pltpu.VMEM((1, rows, keys), cache.dtype),
            pltpu.VMEM((2, 2 * depth, CW), jnp.bfloat16),
            pltpu.VMEM((rows, 2 * depth), jnp.bfloat16),
            pltpu.VMEM((2, rows, CW), jnp.float32),
        ),
        in_specs=[(anywhere,) * len(lists), anywhere, anywhere, vmem, anywhere, vmem, anywhere, vmem],
        out_specs=(vmem,) * 6,
        scratch_shapes=[
            pltpu.VMEM((ng, reps * depth, GW), jnp.bfloat16),
            pltpu.VMEM((reps // 2, rows, 2 * depth), jnp.bfloat16),
            pltpu.VMEM((ng, rows // 2, GW), jnp.float32),
            pltpu.VMEM((2, 2, rows // 2, CW), jnp.float32),
            pltpu.VMEM((rows, feature), jnp.bfloat16),
            pltpu.VMEM((ng, 1, GW), jnp.float32),
            tuple(pltpu.VMEM(x.shape, x.dtype) for x in lists),
            dma((ng,)),
            dma,
            dma((row_chunks + len(lists),)),
            dma((row_chunks + len(lists),)),
            dma((3,)),
            dma((ng,)),
            dma((2, hops)),
            dma((2, hops - 1, ng)),
            dma((2, hops - 1)),
            dma((2, hops - 1, ng)),
            dma((2,)),
            dma((2, nh)),
            dma((2,)),
            dma((2, nh)),
        ],
        compiler_params=pltpu.CompilerParams(
            collective_id=0, has_side_effects=True, vmem_limit_bytes=KERNEL_VMEM
        ),
    )(lists, payload, cache, norm_gain, query_weight, query_bias, kv_weight, kv_bias)
    return tuple(
        pl.pallas_call(
            functools.partial(put_out, row_chunks),
            out_shape=tuple(pltpu.HBM(x.shape, x.dtype) for x in results[:3]),
            in_specs=[vmem] * len(results),
            out_specs=(anywhere,) * 3,
            scratch_shapes=[
                pltpu.VMEM((2, rows, CW), jnp.bfloat16),
                dma((6 * row_chunks,)),
                dma((2,)),
            ],
            compiler_params=pltpu.CompilerParams(vmem_limit_bytes=OUT_VMEM),
        )(*results)
    )


def solution(mesh):
    in_specs = (
        P("section", "rep", None),
        P("section", "rep", None),
        P("section", "rep", None),
        P("section", "rep"),
        P("section", "rep", None),
        P("section", "rep", None),
        P("section", "rep"),
        P("section", None),
        P("section", "rep", None),
        P("section", None),
        P("section", "rep", None),
        P("section", None),
    )
    out_specs = (P("section", "rep", None), P("section", "rep", None), P("section", "rep", None))
    return jax.shard_map(body, mesh=mesh, in_specs=in_specs, out_specs=out_specs, check_vma=False)
```

profile of v0, /device:TPU:0, one launch (start us, length us, event | category | flops | bytes accessed | tf_op | source)
XLA Modules:
  0.0 146.6 jit_solution(3759785967872345820)
XLA Ops:
  1.9 141.2 %shard_map.139 = (bf16[1,512,3584]{2,1,0:T(8,128)(2,1)S(1)}, bf16[1,512,3584]{2,1,0:T(8,128)(2,1)S(1)}, bf16[1,512,1024]{2,1,0:T(8,128)(2,1)S(1)}, bf16[2,896,25...) custom-call(s32[1,128]{1,0:T(1,128)} %bitcast.3, s32[1,2]{1,0:T(1,128)} %bitcast.4, ...), custom_call_target="tpu_custom_call" | custom-call | tf_op jit(solution)/shard_map/pallas_call | solution.py:515
  143.1 3.5 %shard_map.140 = (bf16[1,512,3584]{2,1,0:T(8,128)(2,1)}, bf16[1,512,3584]{2,1,0:T(8,128)(2,1)}, bf16[1,512,1024]{2,1,0:T(8,128)(2,1)}) custom-call(bf16[1,512,3584]{2,1,0:T(8,128)(2,1)S(1)} %get-tuple-element.9.rebuilt_ref, bf16[1,512,3584]{2,1,0:T(8,128)(2,1)S(1)} %get-tuple-element.10.q_ref, bf16[1,512,1024]{2,1,0:T(8,128)(2,1)S(1)} %get-tuple-element.11.kv_ref, ...), custom_call_target="tpu_custom_call" | custom-call | tf_op jit(solution)/shard_map/pallas_call | solution.py:555
where the time goes:
time: 147 us
  Pallas kernels  145 us (99%)
  between operations  1.93 us (1%)
    pallas_call x1, Pallas kernels, body(): pl.pallas_call(functools.partial(kernel, sections, reps, most_blk), out_s...  141 us
    pallas_call x1, Pallas kernels, body(): pl.pallas_call(functools.partial(put_out, row_chunks), out_shape=tuple((p...  3.51 us

commit v1 on v0

--- a/solution.py
+++ b/solution.py
@@ -31,11 +31,11 @@
     lists_ref,
     payload_ref,
     cache_ref,
-    gain_ref,
+    gain_hbm,
     qw_ref,
-    qb_ref,
+    qb_hbm,
     kvw_ref,
-    kvb_ref,
+    kvb_hbm,
     rebuilt_ref,
     q_ref,
     kv_ref,
@@ -47,10 +47,12 @@
     early,
     sums,
     values,
+    gain_ref,
     bias,
     lists,
     local_sem,
     keep_sem,
+    small_sem,
     row_send,
     row_recv,
     own_send,
@@ -122,6 +124,12 @@
         return w.at[c // SLOT, depth_of(block), columns_of(c)]
 
     keep = pltpu.make_async_copy(cache_ref, rebuilt_ref, keep_sem)
+    small = [pltpu.make_async_copy(gain_hbm, gain_ref, small_sem.at[ng])]
+    for g in range(ng):
+        source, first = (qb_hbm, g) if g < ngq else (kvb_hbm, g - ngq)
+        small.append(
+            pltpu.make_async_copy(source.at[:, pl.ds(first * GW, GW)], bias.at[g], small_sem.at[g])
+        )
     own_locals = [
         pltpu.make_async_copy(own(g), slot(g, me), local_sem.at[g]) for g in range(ng)
     ]
@@ -170,6 +178,8 @@
                             list_copy(i).start()
 
             keep.start()
+            for copy in small:
+                copy.start()
 
         pltpu.make_async_remote_copy(
             src_ref=own(g),
@@ -190,10 +200,8 @@
         def _(i):
             values[pl.ds(i * TILE, TILE), :] = jnp.zeros((TILE, feature), values.dtype)
 
-    for g in range(ngq):
-        bias[g] = qb_ref[:, g * GW : (g + 1) * GW]
-    for g in range(ngq, ng):
-        bias[g] = kvb_ref[:, (g - ngq) * GW : (g - ngq + 1) * GW]
+    for copy in small:
+        copy.wait()
     keep.wait()
     for g in range(ng):
         own_locals[g].wait()
@@ -522,7 +530,7 @@
             pltpu.VMEM((rows, 2 * depth), jnp.bfloat16),
             pltpu.VMEM((2, rows, CW), jnp.float32),
         ),
-        in_specs=[(anywhere,) * len(lists), anywhere, anywhere, vmem, anywhere, vmem, anywhere, vmem],
+        in_specs=[(anywhere,) * len(lists)] + [anywhere] * 7,
         out_specs=(vmem,) * 6,
         scratch_shapes=[
             pltpu.VMEM((ng, reps * depth, GW), jnp.bfloat16),
@@ -530,10 +538,12 @@
             pltpu.VMEM((ng, rows // 2, GW), jnp.float32),
             pltpu.VMEM((2, 2, rows // 2, CW), jnp.float32),
             pltpu.VMEM((rows, feature), jnp.bfloat16),
+            pltpu.VMEM(norm_gain.shape, jnp.float32),
             pltpu.VMEM((ng, 1, GW), jnp.float32),
             tuple(pltpu.VMEM(x.shape, x.dtype) for x in lists),
             dma((ng,)),
             dma,
+            dma((ng + 1,)),
             dma((row_chunks + len(lists),)),
             dma((row_chunks + len(lists),)),
             dma((3,)),
@@ -553,13 +563,13 @@
     )(lists, payload, cache, norm_gain, query_weight, query_bias, kv_weight, kv_bias)
     return tuple(
         pl.pallas_call(
-            functools.partial(put_out, row_chunks),
+            functools.partial(put_out, 2),
             out_shape=tuple(pltpu.HBM(x.shape, x.dtype) for x in results[:3]),
             in_specs=[vmem] * len(results),
             out_specs=(anywhere,) * 3,
             scratch_shapes=[
                 pltpu.VMEM((2, rows, CW), jnp.bfloat16),
-                dma((6 * row_chunks,)),
+                dma((6 * 2,)),
                 dma((2,)),
             ],
             compiler_params=pltpu.CompilerParams(vmem_limit_bytes=OUT_VMEM),

time: 147 us -> 146 us (level)
  no operation moved by 1% of the time
where the time goes in v1:
time: 146 us
  Pallas kernels  144 us (99%)
  between operations  1.93 us (1%)
    pallas_call x1, Pallas kernels, body(): pl.pallas_call(functools.partial(kernel, sections, reps, most_blk), out_s...  141 us
    pallas_call x1, Pallas kernels, body(): pl.pallas_call(functools.partial(put_out, 2), out_shape=tuple((pltpu.HBM(...  3.42 us

profile of v1, /device:TPU:0, one launch (start us, length us, event | category | flops | bytes accessed | tf_op | source)
XLA Modules:
  0.0 145.9 jit_solution(4564201035615086758)
XLA Ops:
  1.9 140.6 %shard_map.139 = (bf16[1,512,3584]{2,1,0:T(8,128)(2,1)S(1)}, bf16[1,512,3584]{2,1,0:T(8,128)(2,1)S(1)}, bf16[1,512,1024]{2,1,0:T(8,128)(2,1)S(1)}, bf16[2,896,25...) custom-call(s32[1,128]{1,0:T(1,128)} %bitcast.3, s32[1,2]{1,0:T(1,128)} %bitcast.4, ...), custom_call_target="tpu_custom_call" | custom-call | tf_op jit(solution)/shard_map/pallas_call | solution.py:523
  142.5 3.4 %shard_map.140 = (bf16[1,512,3584]{2,1,0:T(8,128)(2,1)}, bf16[1,512,3584]{2,1,0:T(8,128)(2,1)}, bf16[1,512,1024]{2,1,0:T(8,128)(2,1)}) custom-call(bf16[1,512,3584]{2,1,0:T(8,128)(2,1)S(1)} %get-tuple-element.9.rebuilt_ref, bf16[1,512,3584]{2,1,0:T(8,128)(2,1)S(1)} %get-tuple-element.10.q_ref, bf16[1,512,1024]{2,1,0:T(8,128)(2,1)S(1)} %get-tuple-element.11.kv_ref, ...), custom_call_target="tpu_custom_call" | custom-call | tf_op jit(solution)/shard_map/pallas_call | solution.py:565

commit v2 on v1

--- a/solution.py
+++ b/solution.py
@@ -55,15 +55,13 @@
     small_sem,
     row_send,
     row_recv,
+    list_send,
+    list_recv,
     own_send,
-    pair_own_recv,
-    ring_send,
+    pass_send,
     ring_recv,
-    pair_send,
     pair_recv,
-    far_send,
     far_recv,
-    far_pair_send,
     far_pair_recv,
 ):
     chips = reps // 2
@@ -124,14 +122,15 @@
         return w.at[c // SLOT, depth_of(block), columns_of(c)]
 
     keep = pltpu.make_async_copy(cache_ref, rebuilt_ref, keep_sem)
-    small = [pltpu.make_async_copy(gain_hbm, gain_ref, small_sem.at[ng])]
+    gain_copy = pltpu.make_async_copy(gain_hbm, gain_ref, small_sem.at[0])
+    small = [gain_copy]
     for g in range(ng):
         source, first = (qb_hbm, g) if g < ngq else (kvb_hbm, g - ngq)
         small.append(
-            pltpu.make_async_copy(source.at[:, pl.ds(first * GW, GW)], bias.at[g], small_sem.at[g])
+            pltpu.make_async_copy(source.at[:, pl.ds(first * GW, GW)], bias.at[g], small_sem.at[1])
         )
     own_locals = [
-        pltpu.make_async_copy(own(g), slot(g, me), local_sem.at[g]) for g in range(ng)
+        pltpu.make_async_copy(own(g), slot(g, me), local_sem) for g in range(ng)
     ]
 
     sides = (section + sections - 1) // sections + (2 * sections - 2 - section) // sections
@@ -141,8 +140,8 @@
         return pltpu.make_async_remote_copy(
             src_ref=lists_ref[i],
             dst_ref=lists[i],
-            send_sem=row_send.at[row_chunks + i],
-            recv_sem=row_recv.at[row_chunks + i],
+            send_sem=list_send.at[i],
+            recv_sem=list_recv.at[i],
             device_id={"section": section + 1},
             device_id_type=MESH,
         )
@@ -151,7 +150,7 @@
         return pltpu.make_async_remote_copy(
             src_ref=payload_ref.at[0, pl.ds(j * BLK, BLK), :],
             dst_ref=values.at[pl.ds(j * BLK, BLK), :],
-            send_sem=row_send.at[j],
+            send_sem=row_send,
             recv_sem=row_recv.at[j],
             device_id={"section": section + 1},
             device_id_type=MESH,
@@ -162,8 +161,8 @@
             pltpu.make_async_remote_copy(
                 src_ref=own(g),
                 dst_ref=slot(g, me),
-                send_sem=own_send.at[d],
-                recv_sem=ring_recv.at[d, 0, g],
+                send_sem=own_send,
+                recv_sem=ring_recv.at[0, g],
                 device_id={"rep": towards[d]},
                 device_id_type=MESH,
             ).start()
@@ -184,8 +183,8 @@
         pltpu.make_async_remote_copy(
             src_ref=own(g),
             dst_ref=slot(g, me),
-            send_sem=own_send.at[2],
-            recv_sem=pair_own_recv.at[g],
+            send_sem=own_send,
+            recv_sem=pair_recv.at[g],
             device_id={"rep": partner},
             device_id_type=MESH,
         ).start()
@@ -200,23 +199,23 @@
         def _(i):
             values[pl.ds(i * TILE, TILE), :] = jnp.zeros((TILE, feature), values.dtype)
 
-    for copy in small:
-        copy.wait()
+    def landed(sem, blocks, width=GW, slots=1):
+        part = w.at[pl.ds(0, slots), pl.ds(0, blocks * depth), pl.ds(0, width)]
+        pltpu.make_async_copy(part, part, sem).wait()
+
+    gain_copy.wait()
+    pltpu.make_async_copy(bias, bias, small_sem.at[1]).wait()
     keep.wait()
-    for g in range(ng):
-        own_locals[g].wait()
+    landed(local_sem, 1, slots=ng)
 
     def block_of(d, t, which):
         return rep_at(pos - t if d == 0 else pos + t, which)
 
-    def landed(here, sem):
-        pltpu.make_async_copy(here, here, sem).wait()
-
-    def pass_on(here, send_sem, recv_sem, target):
+    def pass_on(here, recv_sem, target):
         pltpu.make_async_remote_copy(
             src_ref=here,
             dst_ref=here,
-            send_sem=send_sem,
+            send_sem=pass_send,
             recv_sem=recv_sem,
             device_id={"rep": target},
             device_id_type=MESH,
@@ -279,10 +278,7 @@
         return total
 
     def start(g):
-        landed(slot(g, partner), pair_own_recv.at[g])
-        for t in range(1, hops):
-            for e in range(2):
-                landed(slot(g, block_of(e, t, 1 - core)), pair_recv.at[e, t - 1, g])
+        landed(pair_recv.at[g], 2 * hops - 1)
         early[g] = near(g, slice(None), 0)
 
     marks = [(j + 1) * ng // row_chunks for j in range(row_chunks)]
@@ -295,11 +291,11 @@
 
             @pl.loop(done, mark)
             def _(g):
+                landed(ring_recv.at[t - 1, g], 2)
                 for d in range(2):
                     here = slot(g, block_of(d, t, core))
-                    landed(here, ring_recv.at[d, t - 1, g])
                     if t + 1 < hops:
-                        pass_on(here, ring_send.at[d, t - 1], ring_recv.at[d, t, g], towards[d])
+                        pass_on(here, ring_recv.at[t, g], towards[d])
                     else:
                         for k in range(SLOT):
                             c = g * SLOT + k
@@ -309,8 +305,7 @@
                             def _():
                                 pass_on(
                                     piece(c, block_of(d, t, core)),
-                                    far_send.at[d],
-                                    far_recv.at[d, c - d * nh],
+                                    far_recv.at[c - d * nh],
                                     towards[d],
                                 )
 
@@ -325,13 +320,13 @@
                                             pl.ds(k * CW, CW),
                                         ],
                                         dst_ref=last_w.at[d, depth_of(core), :],
-                                        send_sem=far_send.at[d],
-                                        recv_sem=far_recv.at[d, nh - 1],
+                                        send_sem=pass_send,
+                                        recv_sem=far_recv.at[nh - 1],
                                         device_id={"rep": towards[d]},
                                         device_id_type=MESH,
                                     ).start()
 
-                    pass_on(here, pair_send.at[d, t - 1], pair_recv.at[d, t - 1, g], partner)
+                    pass_on(here, pair_recv.at[g], partner)
                 if t + 1 == hops and (t > 1 or done >= ready):
                     for k in range(per_step):
                         other = (g - ready) * per_step + k
@@ -348,11 +343,6 @@
         for d in range(2):
             c = i + d * nh
             sums[i % 2, d] = near(c // SLOT, columns_of(c), half)
-
-    def paired(i):
-        for d in range(2):
-            c = i + d * nh
-            landed(piece(c, block_of(d, hops, 1 - core)), far_pair_recv.at[d, i])
 
     def finish(i):
         for d in range(2):
@@ -375,11 +365,9 @@
                     kv_ref[0, here, pl.ds(pl.multiple_of((c - nq) * CW, CW), CW)] = result
 
     def arrived(i):
+        landed(far_recv.at[i], 2, CW)
         for d in range(2):
-            c = i + d * nh
-            here = piece(c, block_of(d, hops, core))
-            landed(here, far_recv.at[d, i])
-            pass_on(here, far_pair_send.at[d], far_pair_recv.at[d, i], partner)
+            pass_on(piece(i + d * nh, block_of(d, hops, core)), far_pair_recv.at[i], partner)
 
     partial(0)
     last_normed[...] = normed[far]
@@ -397,37 +385,23 @@
         def _():
             partial(i + 1)
 
-        paired(i)
+        landed(far_pair_recv.at[i], 2, CW)
         finish(i)
 
+    landed(far_recv.at[nh - 1], 2, CW)
     for d in range(2):
-        here = last_w.at[d, depth_of(core), :]
-        landed(here, far_recv.at[d, nh - 1])
-        pass_on(here, far_pair_send.at[d], far_pair_recv.at[d, nh - 1], partner)
-
-    def sent(sem, count, width):
-        part = w.at[pl.ds(0, count), pl.ds(0, depth), pl.ds(0, width)]
-        pltpu.make_async_copy(part, part, sem).wait()
-
-    for k in range(3):
-        sent(own_send.at[k], ng, GW)
-    for d in range(2):
-        for t in range(1, hops):
-            if t + 1 < hops:
-                sent(ring_send.at[d, t - 1], ng, GW)
-            sent(pair_send.at[d, t - 1], ng, GW)
-        sent(far_send.at[d], ng, CW)
+        pass_on(last_w.at[d, depth_of(core), :], far_pair_recv.at[nh - 1], partner)
+
+    landed(own_send, 3, slots=ng)
 
     @pl.when(section < sections - 1)
     def _():
         for i in range(len(lists)):
             list_copy(i).wait_send()
-        for j in range(row_chunks):
-            row_copy(j).wait_send()
-
-    for d in range(2):
-        sent(far_pair_send.at[d], ng, CW)
-        landed(last_w.at[d, depth_of(1 - core), :], far_pair_recv.at[d, nh - 1])
+        pltpu.make_async_copy(values, values, row_send).wait()
+
+    landed(pass_send, 4 * hops - 4, slots=ng)
+    landed(far_pair_recv.at[nh - 1], 2, CW)
 
 
 def put_out(
@@ -443,51 +417,42 @@
     kv_out,
     last,
     sem,
-    last_sem,
 ):
     rows = q_ref.shape[1]
     nq = q_ref.shape[2] // CW
     nc = nq + kv_ref.shape[2] // CW
     last_pieces = (nc // 2 - 1, nc - 1)
 
-    copies = []
-
-    def out(source, target, first, stop):
-        step = rows // parts
-        for j in range(parts):
-            here = pl.ds(j * step, step)
-            columns = pl.ds(first, stop - first)
-            copy = pltpu.make_async_copy(
-                source.at[:, here, columns], target.at[:, here, columns], sem.at[len(copies)]
-            )
-            copy.start()
-            copies.append(copy)
-
-    out(rebuilt_ref, rebuilt_out, 0, rebuilt_ref.shape[2])
-    for source, target, base in ((q_ref, q_out, 0), (kv_ref, kv_out, nq)):
-        first = 0
+    step = rows // parts
+
+    def out(source, target, base, k):
         count = source.shape[2] // CW
-        for c in last_pieces:
-            if base <= c < base + count:
-                if c - base > first:
-                    out(source, target, first * CW, (c - base) * CW)
-                first = c - base + 1
-        if first < count:
-            out(source, target, first * CW, count * CW)
-
+        cuts = [c - base for c in last_pieces if base <= c < base + count]
+        for first, stop in zip([0] + [c + 1 for c in cuts], cuts + [count]):
+            if first < stop:
+                columns = pl.ds(first * CW, (stop - first) * CW)
+                for j in range(parts):
+                    here = pl.ds(j * step, step)
+                    pltpu.make_async_copy(
+                        source.at[:, here, columns], target.at[:, here, columns], sem.at[k]
+                    ).start()
+        whole = source.at[:, :, pl.ds(0, (count - len(cuts)) * CW)]
+        return pltpu.make_async_copy(whole, whole, sem.at[k])
+
+    arrays = ((rebuilt_ref, rebuilt_out, nc), (q_ref, q_out, 0), (kv_ref, kv_out, nq))
+    waits = [out(source, target, base, k) for k, (source, target, base) in enumerate(arrays)]
     for d, c in enumerate(last_pieces):
         total = last_sums[d] + jnp.dot(
             last_normed[...], last_w[d], preferred_element_type=jnp.float32
         )
         last[d] = total.astype(jnp.bfloat16)
         target, base = (q_out, 0) if c < nq else (kv_out, nq)
-        copy = pltpu.make_async_copy(
-            last.at[d], target.at[0, :, pl.ds((c - base) * CW, CW)], last_sem.at[d]
-        )
-        copy.start()
-        copies.append(copy)
-    for copy in copies:
+        pltpu.make_async_copy(
+            last.at[d], target.at[0, :, pl.ds((c - base) * CW, CW)], sem.at[len(arrays)]
+        ).start()
+    for copy in waits:
         copy.wait()
+    pltpu.make_async_copy(last, last, sem.at[len(arrays)]).wait()
 
 
 def body(
@@ -541,21 +506,19 @@
             pltpu.VMEM(norm_gain.shape, jnp.float32),
             pltpu.VMEM((ng, 1, GW), jnp.float32),
             tuple(pltpu.VMEM(x.shape, x.dtype) for x in lists),
+            dma,
+            dma,
+            dma((2,)),
+            dma,
+            dma((row_chunks,)),
+            dma((len(lists),)),
+            dma((len(lists),)),
+            dma,
+            dma,
+            dma((hops - 1, ng)),
             dma((ng,)),
-            dma,
-            dma((ng + 1,)),
-            dma((row_chunks + len(lists),)),
-            dma((row_chunks + len(lists),)),
-            dma((3,)),
-            dma((ng,)),
-            dma((2, hops)),
-            dma((2, hops - 1, ng)),
-            dma((2, hops - 1)),
-            dma((2, hops - 1, ng)),
-            dma((2,)),
-            dma((2, nh)),
-            dma((2,)),
-            dma((2, nh)),
+            dma((nh,)),
+            dma((nh,)),
         ],
         compiler_params=pltpu.CompilerParams(
             collective_id=0, has_side_effects=True, vmem_limit_bytes=KERNEL_VMEM
@@ -569,8 +532,7 @@
             out_specs=(anywhere,) * 3,
             scratch_shapes=[
                 pltpu.VMEM((2, rows, CW), jnp.bfloat16),
-                dma((6 * 2,)),
-                dma((2,)),
+                dma((4,)),
             ],
             compiler_params=pltpu.CompilerParams(vmem_limit_bytes=OUT_VMEM),
         )(*results)

time: 146 us -> 145 us (level)
  no operation moved by 1% of the time
where the time goes in v2:
time: 145 us
  Pallas kernels  143 us (99%)
  between operations  1.93 us (1%)
    pallas_call x1, Pallas kernels, body(): pl.pallas_call(functools.partial(kernel, sections, reps, most_blk), out_s...  140 us
    pallas_call x1, Pallas kernels, body(): pl.pallas_call(functools.partial(put_out, 2), out_shape=tuple((pltpu.HBM(...  3.33 us

profile of v2, /device:TPU:0, one launch (start us, length us, event | category | flops | bytes accessed | tf_op | source)
XLA Modules:
  0.0 145.2 jit_solution(12744926063168254061)
XLA Ops:
  1.9 139.9 %shard_map.139 = (bf16[1,512,3584]{2,1,0:T(8,128)(2,1)S(1)}, bf16[1,512,3584]{2,1,0:T(8,128)(2,1)S(1)}, bf16[1,512,1024]{2,1,0:T(8,128)(2,1)S(1)}, bf16[2,896,25...) custom-call(s32[1,128]{1,0:T(1,128)} %bitcast.3, s32[1,2]{1,0:T(1,128)} %bitcast.4, ...), custom_call_target="tpu_custom_call" | custom-call | tf_op jit(solution)/shard_map/pallas_call | solution.py:488
  141.9 3.3 %shard_map.140 = (bf16[1,512,3584]{2,1,0:T(8,128)(2,1)}, bf16[1,512,3584]{2,1,0:T(8,128)(2,1)}, bf16[1,512,1024]{2,1,0:T(8,128)(2,1)}) custom-call(bf16[1,512,3584]{2,1,0:T(8,128)(2,1)S(1)} %get-tuple-element.9.rebuilt_ref, bf16[1,512,3584]{2,1,0:T(8,128)(2,1)S(1)} %get-tuple-element.10.q_ref, bf16[1,512,1024]{2,1,0:T(8,128)(2,1)S(1)} %get-tuple-element.11.kv_ref, ...), custom_call_target="tpu_custom_call" | custom-call | tf_op jit(solution)/shard_map/pallas_call | solution.py:528

commit v3 on v2

--- a/solution.py
+++ b/solution.py
@@ -8,6 +8,7 @@
 from jax.sharding import PartitionSpec as P
 
 BLK = 128
+HALF = 128
 CW = 256
 SLOT = 2
 GW = SLOT * CW
@@ -121,6 +122,9 @@
     def piece(c, block):
         return w.at[c // SLOT, depth_of(block), columns_of(c)]
 
+    def last_part(d, which, p):
+        return last_w.at[d, depth_of(which), pl.ds(p * HALF, HALF)]
+
     keep = pltpu.make_async_copy(cache_ref, rebuilt_ref, keep_sem)
     gain_copy = pltpu.make_async_copy(gain_hbm, gain_ref, small_sem.at[0])
     small = [gain_copy]
@@ -130,11 +134,13 @@
             pltpu.make_async_copy(source.at[:, pl.ds(first * GW, GW)], bias.at[g], small_sem.at[1])
         )
     own_locals = [
-        pltpu.make_async_copy(own(g), slot(g, me), local_sem) for g in range(ng)
+        pltpu.make_async_copy(own(g), slot(g, me), local_sem.at[min(g, 1)]) for g in range(ng)
     ]
 
     sides = (section + sections - 1) // sections + (2 * sections - 2 - section) // sections
+    own_locals[0].start()
     pl.semaphore_wait(barrier, 3 + sides)
+    own_locals[0].wait()
 
     def list_copy(i):
         return pltpu.make_async_remote_copy(
@@ -157,9 +163,10 @@
         )
 
     for g in range(ng):
+        source = own(g) if g else slot(g, me)
         for d in range(2):
             pltpu.make_async_remote_copy(
-                src_ref=own(g),
+                src_ref=source,
                 dst_ref=slot(g, me),
                 send_sem=own_send,
                 recv_sem=ring_recv.at[0, g],
@@ -181,14 +188,15 @@
                 copy.start()
 
         pltpu.make_async_remote_copy(
-            src_ref=own(g),
+            src_ref=source,
             dst_ref=slot(g, me),
             send_sem=own_send,
             recv_sem=pair_recv.at[g],
             device_id={"rep": partner},
             device_id_type=MESH,
         ).start()
-        own_locals[g].start()
+        if g:
+            own_locals[g].start()
 
     @pl.when(section == 0)
     def _():
@@ -206,7 +214,7 @@
     gain_copy.wait()
     pltpu.make_async_copy(bias, bias, small_sem.at[1]).wait()
     keep.wait()
-    landed(local_sem, 1, slots=ng)
+    landed(local_sem.at[1], 1, slots=ng - 1)
 
     def block_of(d, t, which):
         return rep_at(pos - t if d == 0 else pos + t, which)
@@ -313,18 +321,19 @@
 
                                 @pl.when(c == last)
                                 def _():
-                                    pltpu.make_async_remote_copy(
-                                        src_ref=w.at[
-                                            last // SLOT,
-                                            depth_of(block_of(d, t, core)),
-                                            pl.ds(k * CW, CW),
-                                        ],
-                                        dst_ref=last_w.at[d, depth_of(core), :],
-                                        send_sem=pass_send,
-                                        recv_sem=far_recv.at[nh - 1],
-                                        device_id={"rep": towards[d]},
-                                        device_id_type=MESH,
-                                    ).start()
+                                    for p in range(CW // HALF):
+                                        pltpu.make_async_remote_copy(
+                                            src_ref=w.at[
+                                                last // SLOT,
+                                                depth_of(block_of(d, t, core)),
+                                                pl.ds(k * CW + p * HALF, HALF),
+                                            ],
+                                            dst_ref=last_part(d, core, p),
+                                            send_sem=pass_send,
+                                            recv_sem=far_recv.at[nh - 1 + p],
+                                            device_id={"rep": towards[d]},
+                                            device_id_type=MESH,
+                                        ).start()
 
                     pass_on(here, pair_recv.at[g], partner)
                 if t + 1 == hops and (t > 1 or done >= ready):
@@ -388,9 +397,10 @@
         landed(far_pair_recv.at[i], 2, CW)
         finish(i)
 
-    landed(far_recv.at[nh - 1], 2, CW)
-    for d in range(2):
-        pass_on(last_w.at[d, depth_of(core), :], far_pair_recv.at[nh - 1], partner)
+    for p in range(CW // HALF):
+        landed(far_recv.at[nh - 1 + p], 2, HALF)
+        for d in range(2):
+            pass_on(last_part(d, core, p), far_pair_recv.at[nh - 1 + p], partner)
 
     landed(own_send, 3, slots=ng)
 
@@ -401,7 +411,8 @@
         pltpu.make_async_copy(values, values, row_send).wait()
 
     landed(pass_send, 4 * hops - 4, slots=ng)
-    landed(far_pair_recv.at[nh - 1], 2, CW)
+    for p in range(CW // HALF):
+        landed(far_pair_recv.at[nh - 1 + p], 2, HALF)
 
 
 def put_out(
@@ -506,7 +517,7 @@
             pltpu.VMEM(norm_gain.shape, jnp.float32),
             pltpu.VMEM((ng, 1, GW), jnp.float32),
             tuple(pltpu.VMEM(x.shape, x.dtype) for x in lists),
-            dma,
+            dma((2,)),
             dma,
             dma((2,)),
             dma,
@@ -517,8 +528,8 @@
             dma,
             dma((hops - 1, ng)),
             dma((ng,)),
-            dma((nh,)),
-            dma((nh,)),
+            dma((nh - 1 + CW // HALF,)),
+            dma((nh - 1 + CW // HALF,)),
         ],
         compiler_params=pltpu.CompilerParams(
             collective_id=0, has_side_effects=True, vmem_limit_bytes=KERNEL_VMEM

time: 145 us -> 145 us (level)
  no operation moved by 1% of the time
where the time goes in v3:
time: 145 us
  Pallas kernels  143 us (99%)
  between operations  1.93 us (1%)
    pallas_call x1, Pallas kernels, body(): pl.pallas_call(functools.partial(kernel, sections, reps, most_blk), out_s...  139 us
    pallas_call x1, Pallas kernels, body(): pl.pallas_call(functools.partial(put_out, 2), out_shape=tuple((pltpu.HBM(...  3.33 us

profile of v3, /device:TPU:0, one launch (start us, length us, event | category | flops | bytes accessed | tf_op | source)
XLA Modules:
  0.0 144.7 jit_solution(5560185459729094700)
XLA Ops:
  1.9 139.4 %shard_map.139 = (bf16[1,512,3584]{2,1,0:T(8,128)(2,1)S(1)}, bf16[1,512,3584]{2,1,0:T(8,128)(2,1)S(1)}, bf16[1,512,1024]{2,1,0:T(8,128)(2,1)S(1)}, bf16[2,896,25...) custom-call(s32[1,128]{1,0:T(1,128)} %bitcast.3, s32[1,2]{1,0:T(1,128)} %bitcast.4, ...), custom_call_target="tpu_custom_call" | custom-call | tf_op jit(solution)/shard_map/pallas_call | solution.py:499
  141.3 3.3 %shard_map.140 = (bf16[1,512,3584]{2,1,0:T(8,128)(2,1)}, bf16[1,512,3584]{2,1,0:T(8,128)(2,1)}, bf16[1,512,1024]{2,1,0:T(8,128)(2,1)}) custom-call(bf16[1,512,3584]{2,1,0:T(8,128)(2,1)S(1)} %get-tuple-element.9.rebuilt_ref, bf16[1,512,3584]{2,1,0:T(8,128)(2,1)S(1)} %get-tuple-element.10.q_ref, bf16[1,512,1024]{2,1,0:T(8,128)(2,1)S(1)} %get-tuple-element.11.kv_ref, ...), custom_call_target="tpu_custom_call" | custom-call | tf_op jit(solution)/shard_map/pallas_call | solution.py:539

commit v4 on v3

--- a/solution.py
+++ b/solution.py
@@ -10,6 +10,7 @@
 BLK = 128
 HALF = 128
 CW = 256
+PARTS = 2 * CW // HALF
 SLOT = 2
 GW = SLOT * CW
 TILE = 16
@@ -122,8 +123,12 @@
     def piece(c, block):
         return w.at[c // SLOT, depth_of(block), columns_of(c)]
 
+    def half_of(block, p):
+        first = block * depth + p % 2 * (depth // 2)
+        return pl.ds(pl.multiple_of(first, depth // 2), depth // 2)
+
     def last_part(d, which, p):
-        return last_w.at[d, depth_of(which), pl.ds(p * HALF, HALF)]
+        return last_w.at[d, half_of(which, p), pl.ds(p // 2 * HALF, HALF)]
 
     keep = pltpu.make_async_copy(cache_ref, rebuilt_ref, keep_sem)
     gain_copy = pltpu.make_async_copy(gain_hbm, gain_ref, small_sem.at[0])
@@ -321,12 +326,12 @@
 
                                 @pl.when(c == last)
                                 def _():
-                                    for p in range(CW // HALF):
+                                    for p in range(PARTS):
                                         pltpu.make_async_remote_copy(
                                             src_ref=w.at[
                                                 last // SLOT,
-                                                depth_of(block_of(d, t, core)),
-                                                pl.ds(k * CW + p * HALF, HALF),
+                                                half_of(block_of(d, t, core), p),
+                                                pl.ds(k * CW + p // 2 * HALF, HALF),
                                             ],
                                             dst_ref=last_part(d, core, p),
                                             send_sem=pass_send,
@@ -397,8 +402,8 @@
         landed(far_pair_recv.at[i], 2, CW)
         finish(i)
 
-    for p in range(CW // HALF):
-        landed(far_recv.at[nh - 1 + p], 2, HALF)
+    for p in range(PARTS):
+        landed(far_recv.at[nh - 1 + p], 1, HALF)
         for d in range(2):
             pass_on(last_part(d, core, p), far_pair_recv.at[nh - 1 + p], partner)
 
@@ -411,8 +416,8 @@
         pltpu.make_async_copy(values, values, row_send).wait()
 
     landed(pass_send, 4 * hops - 4, slots=ng)
-    for p in range(CW // HALF):
-        landed(far_pair_recv.at[nh - 1 + p], 2, HALF)
+    for p in range(PARTS):
+        landed(far_pair_recv.at[nh - 1 + p], 1, HALF)
 
 
 def put_out(
@@ -528,8 +533,8 @@
             dma,
             dma((hops - 1, ng)),
             dma((ng,)),
-            dma((nh - 1 + CW // HALF,)),
-            dma((nh - 1 + CW // HALF,)),
+            dma((nh - 1 + PARTS,)),
+            dma((nh - 1 + PARTS,)),
         ],
         compiler_params=pltpu.CompilerParams(
             collective_id=0, has_side_effects=True, vmem_limit_bytes=KERNEL_VMEM

time: 145 us -> 145 us (level)
  no operation moved by 1% of the time
where the time goes in v4:
time: 145 us
  Pallas kernels  143 us (99%)
  between operations  1.93 us (1%)
    pallas_call x1, Pallas kernels, body(): pl.pallas_call(functools.partial(kernel, sections, reps, most_blk), out_s...  139 us
    pallas_call x1, Pallas kernels, body(): pl.pallas_call(functools.partial(put_out, 2), out_shape=tuple((pltpu.HBM(...  3.33 us

profile of v4, /device:TPU:0, one launch (start us, length us, event | category | flops | bytes accessed | tf_op | source)
XLA Modules:
  0.0 144.7 jit_solution(5207539687733547313)
XLA Ops:
  1.9 139.4 %shard_map.139 = (bf16[1,512,3584]{2,1,0:T(8,128)(2,1)S(1)}, bf16[1,512,3584]{2,1,0:T(8,128)(2,1)S(1)}, bf16[1,512,1024]{2,1,0:T(8,128)(2,1)S(1)}, bf16[2,896,25...) custom-call(s32[1,128]{1,0:T(1,128)} %bitcast.3, s32[1,2]{1,0:T(1,128)} %bitcast.4, ...), custom_call_target="tpu_custom_call" | custom-call | tf_op jit(solution)/shard_map/pallas_call | solution.py:504
  141.3 3.3 %shard_map.140 = (bf16[1,512,3584]{2,1,0:T(8,128)(2,1)}, bf16[1,512,3584]{2,1,0:T(8,128)(2,1)}, bf16[1,512,1024]{2,1,0:T(8,128)(2,1)}) custom-call(bf16[1,512,3584]{2,1,0:T(8,128)(2,1)S(1)} %get-tuple-element.9.rebuilt_ref, bf16[1,512,3584]{2,1,0:T(8,128)(2,1)S(1)} %get-tuple-element.10.q_ref, bf16[1,512,1024]{2,1,0:T(8,128)(2,1)S(1)} %get-tuple-element.11.kv_ref, ...), custom_call_target="tpu_custom_call" | custom-call | tf_op jit(solution)/shard_map/pallas_call | solution.py:544

commit v5 on v4

--- a/solution.py
+++ b/solution.py
@@ -64,7 +64,6 @@
     ring_recv,
     pair_recv,
     far_recv,
-    far_pair_recv,
 ):
     chips = reps // 2
     hops = chips // 2
@@ -381,7 +380,7 @@
     def arrived(i):
         landed(far_recv.at[i], 2, CW)
         for d in range(2):
-            pass_on(piece(i + d * nh, block_of(d, hops, core)), far_pair_recv.at[i], partner)
+            pass_on(piece(i + d * nh, block_of(d, hops, core)), pair_recv.at[i], partner)
 
     partial(0)
     last_normed[...] = normed[far]
@@ -399,13 +398,13 @@
         def _():
             partial(i + 1)
 
-        landed(far_pair_recv.at[i], 2, CW)
+        landed(pair_recv.at[i], 2, CW)
         finish(i)
 
     for p in range(PARTS):
         landed(far_recv.at[nh - 1 + p], 1, HALF)
         for d in range(2):
-            pass_on(last_part(d, core, p), far_pair_recv.at[nh - 1 + p], partner)
+            pass_on(last_part(d, core, p), pair_recv.at[nh - 1 + p], partner)
 
     landed(own_send, 3, slots=ng)
 
@@ -417,7 +416,7 @@
 
     landed(pass_send, 4 * hops - 4, slots=ng)
     for p in range(PARTS):
-        landed(far_pair_recv.at[nh - 1 + p], 1, HALF)
+        landed(pair_recv.at[nh - 1 + p], 1, HALF)
 
 
 def put_out(
@@ -532,8 +531,7 @@
             dma,
             dma,
             dma((hops - 1, ng)),
-            dma((ng,)),
-            dma((nh - 1 + PARTS,)),
+            dma((max(ng, nh - 1 + PARTS),)),
             dma((nh - 1 + PARTS,)),
         ],
         compiler_params=pltpu.CompilerParams(

time: 145 us -> 145 us (level)
  no operation moved by 1% of the time
where the time goes in v5:
time: 145 us
  Pallas kernels  143 us (99%)
  between operations  1.93 us (1%)
    pallas_call x1, Pallas kernels, body(): pl.pallas_call(functools.partial(kernel, sections, reps, most_blk), out_s...  139 us
    pallas_call x1, Pallas kernels, body(): pl.pallas_call(functools.partial(put_out, 2), out_shape=tuple((pltpu.HBM(...  3.33 us

profile of v5, /device:TPU:0, one launch (start us, length us, event | category | flops | bytes accessed | tf_op | source)
XLA Modules:
  0.0 144.6 jit_solution(4368340927316049484)
XLA Ops:
  1.9 139.3 %shard_map.139 = (bf16[1,512,3584]{2,1,0:T(8,128)(2,1)S(1)}, bf16[1,512,3584]{2,1,0:T(8,128)(2,1)S(1)}, bf16[1,512,1024]{2,1,0:T(8,128)(2,1)S(1)}, bf16[2,896,25...) custom-call(s32[1,128]{1,0:T(1,128)} %bitcast.3, s32[1,2]{1,0:T(1,128)} %bitcast.4, ...), custom_call_target="tpu_custom_call" | custom-call | tf_op jit(solution)/shard_map/pallas_call | solution.py:503
  141.3 3.3 %shard_map.140 = (bf16[1,512,3584]{2,1,0:T(8,128)(2,1)}, bf16[1,512,3584]{2,1,0:T(8,128)(2,1)}, bf16[1,512,1024]{2,1,0:T(8,128)(2,1)}) custom-call(bf16[1,512,3584]{2,1,0:T(8,128)(2,1)S(1)} %get-tuple-element.9.rebuilt_ref, bf16[1,512,3584]{2,1,0:T(8,128)(2,1)S(1)} %get-tuple-element.10.q_ref, bf16[1,512,1024]{2,1,0:T(8,128)(2,1)S(1)} %get-tuple-element.11.kv_ref, ...), custom_call_target="tpu_custom_call" | custom-call | tf_op jit(solution)/shard_map/pallas_call | solution.py:542

commit v6 on v5

--- a/solution.py
+++ b/solution.py
@@ -369,11 +369,11 @@
                 result = total.astype(jnp.bfloat16)
                 here = slice(first, first + half)
 
-                @pl.when(c < nq)
+                @pl.when(jnp.asarray(c < nq))
                 def _():
                     q_ref[0, here, pl.ds(pl.multiple_of(c * CW, CW), CW)] = result
 
-                @pl.when(c >= nq)
+                @pl.when(jnp.asarray(c >= nq))
                 def _():
                     kv_ref[0, here, pl.ds(pl.multiple_of((c - nq) * CW, CW), CW)] = result
 
@@ -390,7 +390,7 @@
         last_sums[d, :half, :] = early[c // SLOT, :, columns]
         last_sums[d, half:, :] = near(c // SLOT, columns, half)
 
-    @pl.loop(0, nh - 1)
+    @pl.loop(0, nh - 2)
     def _(i):
         arrived(i)
 
@@ -401,10 +401,24 @@
         landed(pair_recv.at[i], 2, CW)
         finish(i)
 
-    for p in range(PARTS):
-        landed(far_recv.at[nh - 1 + p], 1, HALF)
-        for d in range(2):
-            pass_on(last_part(d, core, p), pair_recv.at[nh - 1 + p], partner)
+    arrived(nh - 2)
+
+    def pass_last():
+        for p in range(PARTS):
+            landed(far_recv.at[nh - 1 + p], 1, HALF)
+            for d in range(2):
+                pass_on(last_part(d, core, p), pair_recv.at[nh - 1 + p], partner)
+
+    @pl.when(core == 1)
+    def _():
+        pass_last()
+
+    landed(pair_recv.at[nh - 2], 2, CW)
+    finish(nh - 2)
+
+    @pl.when(core == 0)
+    def _():
+        pass_last()
 
     landed(own_send, 3, slots=ng)
 

time: 145 us -> 145 us (level)
  no operation moved by 1% of the time
where the time goes in v6:
time: 145 us; the launch traced here: 144 us
  Pallas kernels  143 us (99%)
  between operations  1.93 us (1%)
    pallas_call x1, Pallas kernels, body(): pl.pallas_call(functools.partial(kernel, sections, reps, most_blk), out_s...  139 us
    pallas_call x1, Pallas kernels, body(): pl.pallas_call(functools.partial(put_out, 2), out_shape=tuple((pltpu.HBM(...  3.33 us

profile of v6, /device:TPU:0, one launch (start us, length us, event | category | flops | bytes accessed | tf_op | source)
XLA Modules:
  0.0 144.5 jit_solution(17503372683601464587)
XLA Ops:
  1.9 139.2 %shard_map.139 = (bf16[1,512,3584]{2,1,0:T(8,128)(2,1)S(1)}, bf16[1,512,3584]{2,1,0:T(8,128)(2,1)S(1)}, bf16[1,512,1024]{2,1,0:T(8,128)(2,1)S(1)}, bf16[2,896,25...) custom-call(s32[1,128]{1,0:T(1,128)} %bitcast.3, s32[1,2]{1,0:T(1,128)} %bitcast.4, ...), custom_call_target="tpu_custom_call" | custom-call | tf_op jit(solution)/shard_map/pallas_call | solution.py:517
  141.2 3.3 %shard_map.140 = (bf16[1,512,3584]{2,1,0:T(8,128)(2,1)}, bf16[1,512,3584]{2,1,0:T(8,128)(2,1)}, bf16[1,512,1024]{2,1,0:T(8,128)(2,1)}) custom-call(bf16[1,512,3584]{2,1,0:T(8,128)(2,1)S(1)} %get-tuple-element.9.rebuilt_ref, bf16[1,512,3584]{2,1,0:T(8,128)(2,1)S(1)} %get-tuple-element.10.q_ref, bf16[1,512,1024]{2,1,0:T(8,128)(2,1)S(1)} %get-tuple-element.11.kv_ref, ...), custom_call_target="tpu_custom_call" | custom-call | tf_op jit(solution)/shard_map/pallas_call | solution.py:556
